TPU v7x, 32 devices: a whole 2x2x4 slice. The times are simulated.
32 devices in a mesh: grp: 2 (over x), dom: 16 (over z, y, core).
Axes of the slice: x: 2, y: 2, z: 4, core: 2. Of those that a mesh axis runs over, the one named last changes fastest.
Arguments:
- surplus: float32 [48, 64, 4096], P('grp', None, 'dom'), may hold values from -40 to 40
- levels: int32 [48, 3], P('grp'), may hold values from 0 to 3
Outputs:
- updated: float32 [48, 64, 4096], P('grp', None, 'dom')
- coefficients: float32 [48], replicated
All inputs are finite; a program needn't handle non-finite values.
Results may differ from a plain program's by a relative error of at most 0.0003.
Values sent between devices are 32-bit elements; how exact they have to be, the bound alone decides.
A program may use at most 64 MiB of HBM per device.

v0:
```python
import jax
import jax.numpy as jnp
from jax import lax
from jax.sharding import PartitionSpec as P


def owned(levels, count):
    indices = jnp.arange(count, dtype=jnp.int32)
    digits = jnp.stack([indices // 16, indices // 4 % 4, indices % 4])
    return jnp.all(digits[None] <= levels[:, :, None], axis=1).astype(jnp.float32)


def solve_weights(gram_matrix):
    number = gram_matrix.shape[0]
    diagonal_part = jnp.diagonal(gram_matrix) + 1e-06
    scaling = 1.0 / jnp.sqrt(diagonal_part)
    system = scaling[:, None] * gram_matrix * scaling[None, :] + 0.1 * jnp.eye(
        number, dtype=jnp.float32
    )
    factor = jnp.linalg.cholesky(system)
    target = jnp.sqrt(diagonal_part)[:, None]
    halfway = lax.linalg.triangular_solve(factor, target, left_side=True, lower=True)
    weights = lax.linalg.triangular_solve(
        factor, halfway, left_side=True, lower=True, transpose_a=True
    )
    return scaling * weights[:, 0]


def inner_rows(left_rows, right_rows):
    return lax.dot_general(
        left_rows,
        right_rows,
        (((1,), (1,)), ((), ())),
        precision=lax.Precision.HIGHEST,
        preferred_element_type=jnp.float32,
    )


def shards(surplus, levels):
    local_count = surplus.shape[0]
    subspaces = surplus.shape[1]
    grid_total = local_count * lax.axis_size("grp")
    owners = owned(levels, subspaces)
    masked = surplus * owners[:, :, None]
    flattened = masked.reshape(local_count, -1)
    portion = lax.all_gather(masked, "grp", axis=0, tiled=True)
    products = inner_rows(flattened, portion.reshape(portion.shape[0], -1))
    row_start = lax.axis_index("grp") * local_count
    placed = lax.dynamic_update_slice(
        jnp.zeros((grid_total, grid_total), jnp.float32), products, (row_start, jnp.int32(0))
    )
    gram_matrix = lax.psum(placed, ("grp", "dom"))
    coefficients = solve_weights(gram_matrix)
    own_weights = lax.dynamic_slice_in_dim(
        coefficients, lax.axis_index("grp") * local_count, local_count
    )
    partial_sum = jnp.tensordot(own_weights, masked, axes=1, precision=lax.Precision.HIGHEST)
    own_share = lax.psum_scatter(partial_sum, "grp", scatter_dimension=0, tiled=True)
    combined = lax.all_gather(own_share, "grp", axis=0, tiled=True)
    updated = owners[:, :, None] * combined[None]
    return (updated, coefficients)


def solution(mesh):
    placed = (P("grp", None, "dom"), P("grp", None))
    return jax.shard_map(
        shards, mesh=mesh, in_specs=placed, out_specs=(P("grp", None, "dom"), P()), check_vma=False
    )
```

profile of v0, /device:TPU:0, one launch (start us, length us, event | category | flops | bytes accessed | tf_op | source)
XLA Modules:
  0.0 140.4 jit_solution(13781790527731997911)
XLA Ops:
  7.2 0.0 all-gather.2.cloned.1.call-start
  7.3 0.8 compare_reduce_fusion
  8.0 0.1 copy.12
  8.1 3.5 %copy_multiply_fusion = f32[24,64,256]{2,0,1:T(8,128)} fusion(f32[24,64,256]{2,1,0:T(8,128)} %param.2, f32[24,64]{0,1:T(8,128)S(1)} %copy.12), kind=kLoop, calls=%fused_computation.1 | loop fusion | flops 393216 | bytes 3151872 | tf_op jit(solution)/shard_map/mul | solution.py:44
  11.6 0.0 reduce-scatter.2.cloned.1.call-start
  11.7 47.7 %all-gather.2.cloned.1.call-done = f32[48,64,256]{2,0,1:T(8,128)} async-done(((f32[24,64,256]{2,0,1:T(8,128)}), f32[48,64,256]{2,0,1:T(8,128)}) %all-gather.2.cloned.1.call-update) | async-done | bytes 3145744 | tf_op jit(solution)/shard_map/all_gather | solution.py:46
  59.4 4.5 %fusion = f32[48,48]{1,0:T(8,128)S(1)} fusion(f32[48,48]{1,0:T(8,128)S(1)} %broadcast_in_dim.5, s32[]{:T(128)S(6)} %select_n.63, f32[24,64,256]{2,0,1:T(8,128)S(1)} %copy-done, f32[48,64,256]{2,0,1:T(8,128)} %all-gather.2.cloned.1.call-done), kind=kOutput, calls=%fused_computation.3 | convolution fusion | flops 226492416 | bytes 4730884 | tf_op jit(solution)/shard_map/dot_general | solution.py:30
  63.9 39.5 %psum.7 = f32[48,48]{1,0:T(8,128)S(1)} all-reduce(f32[48,48]{1,0:T(8,128)S(1)} %fusion), channel_id=1, replica_groups=mesh['grp'=2,'dom'=16] {'grp','dom'}, use_global_device_ids=true, to_apply=%region_1.2 | all-reduce | flops 2304 | bytes 18432 | tf_op jit(solution)/shard_map/psum | solution.py:52
  103.4 1.0 gather_fusion
  104.4 0.1 select_add_fusion
  104.4 0.1 copy.14
  104.5 0.1 fusion.5
  104.6 4.4 %cholesky.16 = f32[48,48]{1,0:T(8,128)S(1)} custom-call(f32[48,48]{1,0:T(8,128)S(1)} %fusion.5), custom_call_target="Cholesky" | custom-call | tf_op jit(solution)/shard_map/jit(cholesky)/cholesky | solution.py:20
  109.0 0.6 compare_reduce_fusion.1
  109.7 0.7 fusion.2
  110.3 3.7 %custom-call.8 = f32[1,48,48]{1,2,0:T(8,128)S(1)} custom-call(f32[1,48,48]{2,1,0:T(8,128)S(1)} %fusion.2), custom_call_target="InvertDiagBlocksLowerTriangular" | custom-call | tf_op jit(solution)/shard_map/triangular_solve | solution.py:23
  114.0 0.1 convolution_bitcast_fusion.2
  114.1 0.2 fusion.1
  114.3 1.0 fusion.7
  115.3 0.6 copy.19
  116.0 10.9 %reduce-scatter.2.cloned.1.call-done = f32[32,256]{1,0:T(8,128)} async-done(((f32[64,256]{1,0:T(8,128)}), f32[32,256]{1,0:T(8,128)}) %reduce-scatter.2.cloned.1.call-update) | async-done | bytes 32784 | tf_op jit(solution)/shard_map/reduce_scatter | solution.py:58
  126.9 4.8 %all_gather.7 = f32[64,256]{1,0:T(8,128)S(1)} all-gather(f32[32,256]{1,0:T(8,128)} %reduce-scatter.2.cloned.1.call-done), channel_id=1, replica_groups=mesh['grp'=2,'dom'=16] {'grp'}, dimensions={0}, use_global_device_ids=true | all-gather | bytes 98304 | tf_op jit(solution)/shard_map/all_gather | solution.py:59
  131.7 0.3 broadcast_multiply_fusion
  131.9 1.6 %copy.15 = f32[24,64,256]{2,1,0:T(8,128)} copy(f32[24,64,256]{2,0,1:T(8,128)S(1)} %broadcast_multiply_fusion) | data formatting | bytes 3145728
  (14 shorter events, 0.1 us)
Async XLA Ops:
  7.2 52.3 %all-gather.2.cloned.1.call-start = ((), (), s32[]{:S(2)}) async-start(), calls=%async_computation.1 | async-start | bytes 4718592 | tf_op jit(solution)/shard_map/all_gather | solution.py:46
  11.6 47.8 %copy-start = (f32[24,64,256]{2,0,1:T(8,128)S(1)}, f32[24,64,256]{2,0,1:T(8,128)}, u32[]{:S(2)}) copy-start(f32[24,64,256]{2,0,1:T(8,128)} %copy_multiply_fusion) | copy-start | bytes 4718596
  11.6 115.2 %reduce-scatter.2.cloned.1.call-start = ((), (), s32[]{:S(2)}) async-start(), calls=%async_computation.2 | async-start | bytes 98304 | tf_op jit(solution)/shard_map/reduce_scatter | solution.py:58
  114.3 17.6 %copy-start.1 = (f32[48]{0:T(128)}, f32[48]{0:T(128)S(1)}, u32[]{:S(2)}) copy-start(f32[48]{0:T(128)S(1)} %fusion.1) | copy-start | bytes 580
Sparse Core Ops, SparseCore 0:
  11.8 47.6 all-gather.1
  116.1 10.7 reduce-scatter.1
where the time goes:
time: 141 us; the launch traced here: 140 us
  waiting for transfers between devices  58.7 us (42%)
  blocking collectives  44.3 us (31%)
  other arithmetic  14.1 us (10%)
  between operations  14.1 us (10%)
  matrix products  5.76 us (4%)
  local copies, waits for them, and re-layouts  3.38 us (2%)
    all_gather x1, waiting for transfers between devices, shards(): portion = lax.all_gather(masked, 'grp', axis=0, tiled=True)  47.7 us
    psum x1, blocking collectives, shards(): gram_matrix = lax.psum(placed, ('grp', 'dom'))  39.5 us
    reduce_scatter x1, waiting for transfers between devices, shards(): lax.psum_scatter(partial_sum, 'grp', scatter_dimension=0, tiled=True)  10.9 us
    another operation x3, other arithmetic, solve_weights(): factor = jnp.linalg.cholesky(system)  5.06 us
    all_gather x1, blocking collectives, shards(): combined = lax.all_gather(own_share, 'grp', axis=0, tiled=True)  4.78 us
    dot_general x1, matrix products, inner_rows(): lax.dot_general(left_rows, right_rows, (((1,), (1,)), ((), ())), precisio...  4.46 us
    another operation x2, other arithmetic, solve_weights(): lax.linalg.triangular_solve(factor, halfway, left_side=True, lower=True,...  4.32 us
    mul x1, other arithmetic, shards(): masked = surplus * owners[:, :, None]  3.5 us
  transfers between devices with their start and end apart: 2, of which 2 were waited for; matrix products, arithmetic and copies ran while one was open for 0% of the time, Pallas kernels for 0%

commit v1 on v0

--- a/solution.py
+++ b/solution.py
@@ -2,6 +2,14 @@
 import jax.numpy as jnp
 from jax import lax
 from jax.sharding import PartitionSpec as P
+
+
+def point_the_face(matrix):
+    across = "dom"
+    along_axis = "grp"
+    for tick in (across, along_axis):
+        matrix = lax.psum(matrix, tick)
+    return matrix
 
 
 def owned(levels, count):
@@ -49,7 +57,7 @@
     placed = lax.dynamic_update_slice(
         jnp.zeros((grid_total, grid_total), jnp.float32), products, (row_start, jnp.int32(0))
     )
-    gram_matrix = lax.psum(placed, ("grp", "dom"))
+    gram_matrix = point_the_face(placed)
     coefficients = solve_weights(gram_matrix)
     own_weights = lax.dynamic_slice_in_dim(
         coefficients, lax.axis_index("grp") * local_count, local_count

time: 141 us -> 166 us (1.18)
  blocking collectives: 44.3 us -> 73.1 us
  waiting for transfers between devices: 58.7 us -> 55.2 us
    psum x1 -> x2, blocking collectives: 39.5 us -> 68.4 us  [point_the_face(): matrix = lax.psum(matrix, tick)]
    reduce_scatter x1, waiting for transfers between devices: 10.9 us -> 7.41 us  [shards(): lax.psum_scatter(partial_sum, 'grp', scatter_dimension=0, tiled=True)]
where the time goes in v1:
time: 166 us
  blocking collectives  73.1 us (44%)
  waiting for transfers between devices  55.2 us (33%)
  other arithmetic  14.2 us (9%)
  between operations  14.1 us (8%)
  matrix products  5.75 us (3%)
  local copies, waits for them, and re-layouts  3.38 us (2%)
    psum x2, blocking collectives, point_the_face(): matrix = lax.psum(matrix, tick)  68.4 us
    all_gather x1, waiting for transfers between devices, shards(): portion = lax.all_gather(masked, 'grp', axis=0, tiled=True)  47.7 us
    reduce_scatter x1, waiting for transfers between devices, shards(): lax.psum_scatter(partial_sum, 'grp', scatter_dimension=0, tiled=True)  7.41 us
    another operation x3, other arithmetic, solve_weights(): factor = jnp.linalg.cholesky(system)  5.06 us
    all_gather x1, blocking collectives, shards(): combined = lax.all_gather(own_share, 'grp', axis=0, tiled=True)  4.78 us
    dot_general x1, matrix products, inner_rows(): lax.dot_general(left_rows, right_rows, (((1,), (1,)), ((), ())), precisio...  4.46 us
    another operation x2, other arithmetic, solve_weights(): lax.linalg.triangular_solve(factor, halfway, left_side=True, lower=True,...  4.34 us
    mul x1, other arithmetic, shards(): masked = surplus * owners[:, :, None]  3.5 us
  transfers between devices with their start and end apart: 2, of which 2 were waited for; matrix products, arithmetic and copies ran while one was open for 0% of the time, Pallas kernels for 0%

profile of v1, /device:TPU:0, one launch (start us, length us, event | category | flops | bytes accessed | tf_op | source)
XLA Modules:
  0.0 165.8 jit_solution(12551827892473646628)
XLA Ops:
  7.3 0.8 compare_reduce_fusion
  8.0 0.1 copy.12
  8.1 3.5 %copy_multiply_fusion = f32[24,64,256]{2,0,1:T(8,128)} fusion(f32[24,64,256]{2,1,0:T(8,128)} %param.2, f32[24,64]{0,1:T(8,128)S(1)} %copy.12), kind=kLoop, calls=%fused_computation.1 | loop fusion | flops 393216 | bytes 3151872 | tf_op jit(solution)/shard_map/mul | solution.py:52
  11.6 0.0 reduce-scatter.2.cloned.1.call-start
  11.7 47.7 %all-gather.2.cloned.1.call-done = f32[48,64,256]{2,0,1:T(8,128)} async-done(((f32[24,64,256]{2,0,1:T(8,128)}), f32[48,64,256]{2,0,1:T(8,128)}) %all-gather.2.cloned.1.call-update) | async-done | bytes 3145744 | tf_op jit(solution)/shard_map/all_gather | solution.py:54
  59.4 4.5 %fusion = f32[48,48]{1,0:T(8,128)S(1)} fusion(f32[48,48]{1,0:T(8,128)S(1)} %broadcast_in_dim.5, s32[]{:T(128)S(6)} %select_n.63, f32[24,64,256]{2,0,1:T(8,128)S(1)} %copy-done, f32[48,64,256]{2,0,1:T(8,128)} %all-gather.2.cloned.1.call-done), kind=kOutput, calls=%fused_computation.3 | convolution fusion | flops 226492416 | bytes 4730884 | tf_op jit(solution)/shard_map/dot_general | solution.py:38
  63.9 61.0 %psum.14 = f32[48,48]{1,0:T(8,128)S(1)} all-reduce(f32[48,48]{1,0:T(8,128)S(1)} %fusion), channel_id=1, replica_groups=mesh['grp'=2,'dom'=16] {'dom'}, use_global_device_ids=true, to_apply=%region_1.2 | all-reduce | flops 2304 | bytes 18432 | tf_op jit(solution)/shard_map/psum | solution.py:11
  124.9 7.3 %psum.15 = f32[48,48]{1,0:T(8,128)S(1)} all-reduce(f32[48,48]{1,0:T(8,128)S(1)} %psum.14), channel_id=1, replica_groups=mesh['grp'=2,'dom'=16] {'grp'}, use_global_device_ids=true, to_apply=%region_2.3 | all-reduce | flops 2304 | bytes 18432 | tf_op jit(solution)/shard_map/psum | solution.py:11
  132.3 1.0 gather_fusion
  133.2 0.1 select_add_fusion
  133.3 0.1 copy.14
  133.4 0.1 fusion.5
  133.5 4.4 %cholesky.16 = f32[48,48]{1,0:T(8,128)S(1)} custom-call(f32[48,48]{1,0:T(8,128)S(1)} %fusion.5), custom_call_target="Cholesky" | custom-call | tf_op jit(solution)/shard_map/jit(cholesky)/cholesky | solution.py:28
  137.9 0.6 compare_reduce_fusion.1
  138.5 0.7 fusion.2
  139.2 3.7 %custom-call.8 = f32[1,48,48]{1,2,0:T(8,128)S(1)} custom-call(f32[1,48,48]{2,1,0:T(8,128)S(1)} %fusion.2), custom_call_target="InvertDiagBlocksLowerTriangular" | custom-call | tf_op jit(solution)/shard_map/triangular_solve | solution.py:31
  142.9 0.1 convolution_bitcast_fusion.2
  143.0 0.1 fusion.1
  143.2 1.0 fusion.7
  144.2 0.6 copy.19
  144.8 7.4 %reduce-scatter.2.cloned.1.call-done = f32[32,256]{1,0:T(8,128)} async-done(((f32[64,256]{1,0:T(8,128)}), f32[32,256]{1,0:T(8,128)}) %reduce-scatter.2.cloned.1.call-update) | async-done | bytes 32784 | tf_op jit(solution)/shard_map/reduce_scatter | solution.py:66
  152.2 4.8 %all_gather.7 = f32[64,256]{1,0:T(8,128)S(1)} all-gather(f32[32,256]{1,0:T(8,128)} %reduce-scatter.2.cloned.1.call-done), channel_id=1, replica_groups=mesh['grp'=2,'dom'=16] {'grp'}, dimensions={0}, use_global_device_ids=true | all-gather | bytes 98304 | tf_op jit(solution)/shard_map/all_gather | solution.py:67
  157.0 0.3 broadcast_multiply_fusion
  157.3 1.6 copy.15
  (15 shorter events, 0.2 us)
Async XLA Ops:
  7.2 52.3 %all-gather.2.cloned.1.call-start = ((), (), s32[]{:S(2)}) async-start(), calls=%async_computation.1 | async-start | bytes 4718592 | tf_op jit(solution)/shard_map/all_gather | solution.py:54
  11.6 47.8 %copy-start = (f32[24,64,256]{2,0,1:T(8,128)S(1)}, f32[24,64,256]{2,0,1:T(8,128)}, u32[]{:S(2)}) copy-start(f32[24,64,256]{2,0,1:T(8,128)} %copy_multiply_fusion) | copy-start | bytes 4718596
  11.6 140.6 %reduce-scatter.2.cloned.1.call-start = ((), (), s32[]{:S(2)}) async-start(), calls=%async_computation.2 | async-start | bytes 98304 | tf_op jit(solution)/shard_map/reduce_scatter | solution.py:66
  143.2 14.1 %copy-start.1 = (f32[48]{0:T(128)}, f32[48]{0:T(128)S(1)}, u32[]{:S(2)}) copy-start(f32[48]{0:T(128)S(1)} %fusion.1) | copy-start | bytes 580
Sparse Core Ops, SparseCore 0:
  11.8 47.6 all-gather.1
  144.9 7.2 reduce-scatter.1
